TPU v7x, 32 devices: a whole 2x2x4 slice. The times are simulated.
32 devices in a mesh: gx: 2 (over x), gy: 4 (over y, core), gz: 4 (over z).
Axes of the slice: x: 2, y: 2, z: 4, core: 2. Of those that a mesh axis runs over, the one named last changes fastest.
Arguments:
- rhs: float32 [8, 8, 2, 16, 512], P(None, None, 'gx', 'gy', 'gz'), as said below
- blocks: bfloat16 [7, 8, 8, 2, 16, 512], P(None, None, None, 'gx', 'gy', 'gz'), as said below
Outputs:
- basis: float32 [4, 8, 8, 2, 16, 512], P(None, None, None, 'gx', 'gy', 'gz')
- hess: float32 [4, 8, 3, 8], replicated
Inputs may be any that keep to these rules, and one draw needn't show every extreme that they name: `rhs`: each cell's value is a random draw times a positive scale that varies smoothly over the grid. The operator couples each cell only to itself and its six face neighbours; its blocks are full and the block Krylov spaces keep full rank.
All inputs are finite; a program needn't handle non-finite values.
Results may differ from a plain program's by a relative error of at most 0.001.
Values sent between devices are 32-bit elements; how exact they have to be, the bound alone decides.
A program may use at most 64 MiB of HBM per device.

v0:
```python
import jax
import jax.numpy as jnp
from jax import lax
from jax.sharding import PartitionSpec as P

RHS = 8
ITERS = 3
HIGH = lax.Precision.HIGHEST


def with_halo(block, sides, width):
    for axis, dim in sides:
        count = lax.axis_size(axis)
        forward = [(i, i + 1) for i in range(count - 1)]
        backward = [(target, source) for source, target in forward]
        low = lax.ppermute(
            lax.slice_in_dim(block, block.shape[dim] - width, None, axis=dim), axis, forward
        )
        high = lax.ppermute(lax.slice_in_dim(block, 0, width, axis=dim), axis, backward)
        block = jnp.concatenate([low, block, high], axis=dim)
    return block


def couple(padded, blocks):
    views = [
        padded[:, :, 1:-1, 1:-1, 1:-1],
        padded[:, :, 2:, 1:-1, 1:-1],
        padded[:, :, :-2, 1:-1, 1:-1],
        padded[:, :, 1:-1, 2:, 1:-1],
        padded[:, :, 1:-1, :-2, 1:-1],
        padded[:, :, 1:-1, 1:-1, 2:],
        padded[:, :, 1:-1, 1:-1, :-2],
    ]
    total = jnp.zeros(views[0].shape, jnp.float32)
    for k in range(7):
        for j in range(views[0].shape[0]):
            column = blocks[k, :, j].astype(jnp.float32)
            total = total + column[:, None] * views[k][j][None]
    return total


def stencil(field, blocks):
    padded = with_halo(field, (("gx", 2), ("gy", 3), ("gz", 4)), 1)
    return couple(padded, blocks)


def pair(first, second):
    return jnp.einsum("arxyz,asxyz->rs", first, second, precision=HIGH)


def mix(field, matrix):
    return jnp.einsum("asxyz,sr->arxyz", field, matrix, precision=HIGH)


def normalizer(gram, eye):
    lower = jnp.linalg.cholesky(gram)
    inverse = lax.linalg.triangular_solve(lower, eye, left_side=True, lower=True)
    return (inverse.T, lower.T)


def shards(rhs, blocks):
    eye = jnp.eye(RHS, dtype=jnp.float32)
    hess = jnp.zeros((ITERS + 1, RHS, ITERS, RHS), jnp.float32)
    first_pair = None
    raw_image = stencil(rhs, blocks)
    gram_start, cross, square = lax.psum(
        (pair(rhs, rhs), pair(rhs, raw_image), pair(raw_image, raw_image)), ("gx", "gy", "gz")
    )
    scale, upper = normalizer(gram_start, eye)
    basis = [mix(rhs, scale)]
    images = [mix(raw_image, scale)]
    first_coeff = jnp.dot(jnp.dot(scale.T, cross, precision=HIGH), scale, precision=HIGH)
    first_gram = jnp.dot(jnp.dot(scale.T, square, precision=HIGH), scale, precision=HIGH)
    first_pair = (first_coeff, first_gram)
    for step in range(ITERS):
        image = images[step]
        if step == 0 and first_pair is not None:
            coeffs = [first_pair[0]]
            gram = first_pair[1]
        else:
            stacked = jnp.stack(basis + [image])
            partial_sums = jnp.einsum("karxyz,asxyz->krs", stacked, image, precision=HIGH)
            summed = lax.psum(partial_sums, ("gx", "gy", "gz"))
            coeffs = [summed[index] for index in range(len(basis))]
            gram = summed[len(basis)]
        rest = image
        for vector, coeff in zip(basis, coeffs):
            gram = gram - jnp.dot(coeff.T, coeff, precision=HIGH)
            rest = rest - mix(vector, coeff)
        scale, upper = normalizer(gram, eye)
        fresh = mix(rest, scale)
        basis.append(fresh)
        for index, coeff in enumerate(coeffs):
            hess = hess.at[index, :, step, :].set(coeff)
        hess = hess.at[step + 1, :, step, :].set(upper)
        if step + 1 < ITERS:
            images.append(stencil(fresh, blocks))
    return (jnp.stack(basis), hess)


def solution(mesh):
    placed = (P(None, None, "gx", "gy", "gz"), P(None, None, None, "gx", "gy", "gz"))
    return jax.shard_map(
        shards,
        mesh=mesh,
        in_specs=placed,
        out_specs=(P(None, None, None, "gx", "gy", "gz"), P()),
        check_vma=False,
    )
```

profile of v0, /device:TPU:0, one launch (start us, length us, event | category | flops | bytes accessed | tf_op | source)
XLA Modules:
  0.0 246.0 jit_solution(17078392354189909345)
XLA Ops:
  0.6 1.0 copy.203
  1.6 4.9 %collective-permute-start.1 = (f32[8,8,1,4,128]{4,1,3,2,0:T(8,128)S(1)}, f32[8,8,1,4,128]{4,1,3,2,0:T(8,128)S(1)}, u32[]{:S(2)}, u32[]{:S(2)}) collective-permute-start(f32[8,8,1,4,128]{4,1,3,2,0:T(8,128)S(1)} %copy.203), channel_id=1, source_target_pairs={{0,16},{1,17},{2,18},{3,19},{4,20},{5,21},{6,22},{7,23},{8,24},{9,... | collective-permute-start | bytes 393224 | tf_op jit(solution)/shard_map/ppermute | solution.py:16
  6.5 1.3 collective-permute-start
  7.8 0.9 bitcast_convert_fusion.53
  10.2 3.1 %collective-permute-done = f32[8,8,1,4,128]{4,1,3,2,0:T(8,128)S(1)} collective-permute-done((f32[8,8,1,4,128]{4,1,3,2,0:T(8,128)S(1)}, f32[8,8,1,4,128]{4,1,3,2,0:T(8,128)S(1)}, u32[]{:S(2)}, u32[]{:S(2)}) %collective-permute-start) | collective-permute-done | bytes 131104 | tf_op jit(solution)/shard_map/ppermute | solution.py:19
  13.4 1.3 collective-permute-start.2
  14.7 3.0 %collective-permute-start.3 = (f32[8,8,3,1,128]{4,1,3,2,0:T(8,128)S(1)}, f32[8,8,3,1,128]{4,1,3,2,0:T(8,128)S(1)}, u32[]{:S(2)}, u32[]{:S(2)}) collective-permute-start(f32[8,8,3,1,128]{4,1,3,2,0:T(8,128)S(1)} %get-tuple-element.285), channel_id=1, source_target_pairs={{0,4},{4,8},{8,12},{1,5},{5,9},{9,13},{2,6},{6,10},{10,14},{3,7},{... | collective-permute-start | bytes 294920 | tf_op jit(solution)/shard_map/ppermute | solution.py:16
  18.9 0.9 copy.278
  19.8 3.5 %collective-permute-start.5 = (f32[8,8,3,6,1]{1,0,4,3,2:T(8,128)S(1)}, f32[8,8,3,6,1]{1,0,4,3,2:T(8,128)S(1)}, u32[]{:S(2)}, u32[]{:S(2)}) collective-permute-start(f32[8,8,3,6,1]{1,0,4,3,2:T(8,128)S(1)} %copy.278), channel_id=1, source_target_pairs={{0,1},{1,2},{2,3},{4,5},{5,6},{6,7},{8,9},{9,10},{10,11},{12,13},{... | collective-permute-start | bytes 13832 | tf_op jit(solution)/shard_map/ppermute | solution.py:16
  24.2 1.3 collective-permute-start.4
  25.6 0.9 copy.209
  26.7 4.0 %collective-permute-done.4 = f32[8,8,3,6,1]{1,0,4,3,2:T(8,128)S(1)} collective-permute-done((f32[8,8,3,6,1]{1,0,4,3,2:T(8,128)S(1)}, f32[8,8,3,6,1]{1,0,4,3,2:T(8,128)S(1)}, u32[]{:S(2)}, u32[]{:S(2)}) %collective-permute-start.4) | collective-permute-done | bytes 4640 | tf_op jit(solution)/shard_map/ppermute | solution.py:19
  30.7 0.9 copy.207
  31.8 1.0 multiply_add_fusion.2
  33.6 41.6 %all-reduce.1 = (f32[8,8]{0,1:T(8,128)S(1)}, f32[8,8]{1,0:T(8,128)S(1)}, f32[8,8]{0,1:T(8,128)S(1)}) all-reduce(f32[8,8]{0,1:T(8,128)S(1)} %convolution_bitcast_fusion.13, f32[8,8]{1,0:T(8,128)S(1)} %convolution_bitcast_fusion.12, f32[8,8]{0,1:T(8,128)S(1)} %convolution_bitcast_fusion.11), channel_id=1, replica_groups=mesh['gx'=2,'gy'=4,'gz'=4] {'gx','gy','gz'}, use_global_device_ids=true, to_apply=%region_0.0 | all-reduce | flops 192 | bytes 1536 | tf_op jit(solution)/shard_map/psum | solution.py:66
  83.0 1.3 collective-permute-start.6
  84.3 4.6 %collective-permute-start.7 = (f32[8,8,1,4,128]{4,1,3,0,2:T(8,128)S(1)}, f32[8,8,1,4,128]{4,1,3,0,2:T(8,128)S(1)}, u32[]{:S(2)}, u32[]{:S(2)}) collective-permute-start(f32[8,8,1,4,128]{4,1,3,0,2:T(8,128)S(1)} %bitcast.786), channel_id=1, source_target_pairs={{0,16},{1,17},{2,18},{3,19},{4,20},{5,21},{6,22},{7,23},{8,24},{9,... | collective-permute-start | bytes 393224 | tf_op jit(solution)/shard_map/ppermute | solution.py:16
  90.8 2.8 %and_reduce_fusion = (pred[]{:T(512)}, pred[]{:T(512)}) fusion(s32[4]{0:T(128)S(1)} %copy-done.3, s32[1]{0:T(128)} %constant.288.clone.1, s32[1]{0:T(128)} %get-tuple-element.366, s32[1]{0:T(128)} %get-tuple-element.365, s32[1]{0:T(128)} %slice.1472, s32[1]{0:T(128)S(1)} %bitcast.825), kind=kLoop, calls=%fused_computation.849 | loop fusion | flops 54 | bytes 38 | tf_op jit(solution)/shard_map/reduce.18
  93.7 1.3 collective-permute-start.8
  95.0 3.0 %collective-permute-start.9 = (f32[8,8,3,1,128]{4,1,3,0,2:T(8,128)S(1)}, f32[8,8,3,1,128]{4,1,3,0,2:T(8,128)S(1)}, u32[]{:S(2)}, u32[]{:S(2)}) collective-permute-start(f32[8,8,3,1,128]{4,1,3,0,2:T(8,128)S(1)} %get-tuple-element.283), channel_id=1, source_target_pairs={{0,4},{4,8},{8,12},{1,5},{5,9},{9,13},{2,6},{6,10},{10,14},{3,7},{... | collective-permute-start | bytes 294920 | tf_op jit(solution)/shard_map/ppermute | solution.py:16
  99.2 0.9 copy.218
  100.1 2.2 collective-permute-start.11
  103.2 1.3 collective-permute-start.10
  104.6 0.9 copy.219
  105.7 3.7 %collective-permute-done.10 = f32[8,8,3,6,1]{1,0,4,3,2:T(8,128)S(1)} collective-permute-done((f32[8,8,3,6,1]{1,0,4,3,2:T(8,128)S(1)}, f32[8,8,3,6,1]{1,0,4,3,2:T(8,128)S(1)}, u32[]{:S(2)}, u32[]{:S(2)}) %collective-permute-start.10) | collective-permute-done | bytes 4640 | tf_op jit(solution)/shard_map/ppermute | solution.py:19
  109.4 0.9 copy.217
  110.6 1.1 multiply_add_fusion.1
  111.7 1.6 convolution_bitcast_fusion.7
  113.3 42.8 %psum.38 = f32[3,8,8]{2,1,0:T(8,128)S(1)} all-reduce(f32[3,8,8]{2,1,0:T(8,128)S(1)} %convolution_bitcast_fusion.7), channel_id=1, replica_groups=mesh['gx'=2,'gy'=4,'gz'=4] {'gx','gy','gz'}, use_global_device_ids=true, to_apply=%region_5.8 | all-reduce | flops 192 | bytes 1536 | tf_op jit(solution)/shard_map/psum | solution.py:83
  159.8 1.3 fusion.3
  161.4 1.3 collective-permute-start.12
  162.7 4.6 %collective-permute-start.13 = (f32[8,8,1,4,128]{4,1,3,0,2:T(8,128)S(1)}, f32[8,8,1,4,128]{4,1,3,0,2:T(8,128)S(1)}, u32[]{:S(2)}, u32[]{:S(2)}) collective-permute-start(f32[8,8,1,4,128]{4,1,3,0,2:T(8,128)S(1)} %bitcast.803), channel_id=1, source_target_pairs={{0,16},{1,17},{2,18},{3,19},{4,20},{5,21},{6,22},{7,23},{8,24},{9,... | collective-permute-start | bytes 393224 | tf_op jit(solution)/shard_map/ppermute | solution.py:16
  167.3 1.3 fusion.499
  168.7 1.1 collective-permute-done.13
  169.8 1.3 collective-permute-start.14
  171.1 3.0 %collective-permute-start.15 = (f32[8,8,3,1,128]{4,1,3,0,2:T(8,128)S(1)}, f32[8,8,3,1,128]{4,1,3,0,2:T(8,128)S(1)}, u32[]{:S(2)}, u32[]{:S(2)}) collective-permute-start(f32[8,8,3,1,128]{4,1,3,0,2:T(8,128)S(1)} %get-tuple-element.281), channel_id=1, source_target_pairs={{0,4},{4,8},{8,12},{1,5},{5,9},{9,13},{2,6},{6,10},{10,14},{3,7},{... | collective-permute-start | bytes 294920 | tf_op jit(solution)/shard_map/ppermute | solution.py:16
  175.3 0.9 copy.230
  176.2 2.2 collective-permute-start.17
  179.3 1.3 collective-permute-start.16
  180.7 0.9 copy.231
  181.8 3.7 %collective-permute-done.16 = f32[8,8,3,6,1]{1,0,4,3,2:T(8,128)S(1)} collective-permute-done((f32[8,8,3,6,1]{1,0,4,3,2:T(8,128)S(1)}, f32[8,8,3,6,1]{1,0,4,3,2:T(8,128)S(1)}, u32[]{:S(2)}, u32[]{:S(2)}) %collective-permute-start.16) | collective-permute-done | bytes 4640 | tf_op jit(solution)/shard_map/ppermute | solution.py:19
  185.5 0.9 copy.229
  186.7 1.0 multiply_add_fusion
  187.8 1.6 convolution_bitcast_fusion.6
  189.4 44.9 %psum.39 = f32[4,8,8]{2,1,0:T(8,128)S(1)} all-reduce(f32[4,8,8]{2,1,0:T(8,128)S(1)} %convolution_bitcast_fusion.6), channel_id=1, replica_groups=mesh['gx'=2,'gy'=4,'gz'=4] {'gx','gy','gz'}, use_global_device_ids=true, to_apply=%region_6.9 | all-reduce | flops 256 | bytes 2048 | tf_op jit(solution)/shard_map/psum | solution.py:83
  238.6 1.1 fusion.7
  240.0 0.9 copy.245
  240.9 3.3 %fusion.498 = f32[4,8,3,8]{3,1,2,0:T(8,128)} fusion(f32[4,8,3,8]{3,1,2,0:T(8,128)} %copy-done.2, s32[]{:T(128)} %bitcast.379, s32[]{:T(128)} %bitcast.380, f32[4,8,8]{2,1,0:T(8,128)S(1)} %psum.39, pred[]{:T(512)} %get-tuple-element.118), kind=kLoop, calls=%fused_computation.797 | loop fusion | flops 64 | bytes 9984 | tf_op jit(solution)/shard_map/scatter | solution.py:94
  (149 shorter events, 30.1 us)
Async XLA Ops:
  0.6 8.1 %copy-start.1 = (bf16[7,8,8,1,4,128]{5,4,3,2,1,0:T(4,128)(2,1)S(1)}, bf16[7,8,8,1,4,128]{5,4,3,2,1,0:T(4,128)(2,1)}, u32[]{:S(2)}) copy-start(bf16[7,8,8,1,4,128]{5,4,3,2,1,0:T(4,128)(2,1)} %param.24) | copy-start | bytes 1376260
  1.6 8.5 %collective-permute-start.1 = (f32[8,8,1,4,128]{4,1,3,2,0:T(8,128)S(1)}, f32[8,8,1,4,128]{4,1,3,2,0:T(8,128)S(1)}, u32[]{:S(2)}, u32[]{:S(2)}) collective-permute-start(f32[8,8,1,4,128]{4,1,3,2,0:T(8,128)S(1)} %copy.203), channel_id=1, source_target_pairs={{0,16},{1,17},{2,18},{3,19},{4,20},{5,21},{6,22},{7,23},{8,24},{9,... | collective-permute-start | bytes 393224 | tf_op jit(solution)/shard_map/ppermute | solution.py:16
  6.5 6.9 %collective-permute-start = (f32[8,8,1,4,128]{4,1,3,2,0:T(8,128)S(1)}, f32[8,8,1,4,128]{4,1,3,2,0:T(8,128)S(1)}, u32[]{:S(2)}, u32[]{:S(2)}) collective-permute-start(f32[8,8,1,4,128]{4,1,3,2,0:T(8,128)S(1)} %copy.203), channel_id=1, source_target_pairs={{16,0},{17,1},{18,2},{19,3},{20,4},{21,5},{22,6},{23,7},{24,8},{25... | collective-permute-start | bytes 393224 | tf_op jit(solution)/shard_map/ppermute | solution.py:19
  8.8 0.9 copy-start
  13.4 4.4 %collective-permute-start.2 = (f32[8,8,3,1,128]{4,1,3,2,0:T(8,128)S(1)}, f32[8,8,3,1,128]{4,1,3,2,0:T(8,128)S(1)}, u32[]{:S(2)}, u32[]{:S(2)}) collective-permute-start(f32[8,8,3,1,128]{4,1,3,2,0:T(8,128)S(1)} %get-tuple-element.286), channel_id=1, source_target_pairs={{4,0},{8,4},{12,8},{5,1},{9,5},{13,9},{6,2},{10,6},{14,10},{7,3},{... | collective-permute-start | bytes 294920 | tf_op jit(solution)/shard_map/ppermute | solution.py:19
  14.7 4.0 %collective-permute-start.3 = (f32[8,8,3,1,128]{4,1,3,2,0:T(8,128)S(1)}, f32[8,8,3,1,128]{4,1,3,2,0:T(8,128)S(1)}, u32[]{:S(2)}, u32[]{:S(2)}) collective-permute-start(f32[8,8,3,1,128]{4,1,3,2,0:T(8,128)S(1)} %get-tuple-element.285), channel_id=1, source_target_pairs={{0,4},{4,8},{8,12},{1,5},{5,9},{9,13},{2,6},{6,10},{10,14},{3,7},{... | collective-permute-start | bytes 294920 | tf_op jit(solution)/shard_map/ppermute | solution.py:16
  19.8 5.7 %collective-permute-start.5 = (f32[8,8,3,6,1]{1,0,4,3,2:T(8,128)S(1)}, f32[8,8,3,6,1]{1,0,4,3,2:T(8,128)S(1)}, u32[]{:S(2)}, u32[]{:S(2)}) collective-permute-start(f32[8,8,3,6,1]{1,0,4,3,2:T(8,128)S(1)} %copy.278), channel_id=1, source_target_pairs={{0,1},{1,2},{2,3},{4,5},{5,6},{6,7},{8,9},{9,10},{10,11},{12,13},{... | collective-permute-start | bytes 13832 | tf_op jit(solution)/shard_map/ppermute | solution.py:16
  24.2 6.5 %collective-permute-start.4 = (f32[8,8,3,6,1]{1,0,4,3,2:T(8,128)S(1)}, f32[8,8,3,6,1]{1,0,4,3,2:T(8,128)S(1)}, u32[]{:S(2)}, u32[]{:S(2)}) collective-permute-start(f32[8,8,3,6,1]{1,0,4,3,2:T(8,128)S(1)} %copy.277), channel_id=1, source_target_pairs={{1,0},{2,1},{3,2},{5,4},{6,5},{7,6},{9,8},{10,9},{11,10},{13,12},{... | collective-permute-start | bytes 13832 | tf_op jit(solution)/shard_map/ppermute | solution.py:19
  83.0 10.6 %collective-permute-start.6 = (f32[8,8,1,4,128]{4,1,3,0,2:T(8,128)S(1)}, f32[8,8,1,4,128]{4,1,3,0,2:T(8,128)S(1)}, u32[]{:S(2)}, u32[]{:S(2)}) collective-permute-start(f32[8,8,1,4,128]{4,1,3,0,2:T(8,128)S(1)} %bitcast.785), channel_id=1, source_target_pairs={{16,0},{17,1},{18,2},{19,3},{20,4},{21,5},{22,6},{23,7},{24,8},{25... | collective-permute-start | bytes 393224 | tf_op jit(solution)/shard_map/ppermute | solution.py:19
  84.3 9.3 %collective-permute-start.7 = (f32[8,8,1,4,128]{4,1,3,0,2:T(8,128)S(1)}, f32[8,8,1,4,128]{4,1,3,0,2:T(8,128)S(1)}, u32[]{:S(2)}, u32[]{:S(2)}) collective-permute-start(f32[8,8,1,4,128]{4,1,3,0,2:T(8,128)S(1)} %bitcast.786), channel_id=1, source_target_pairs={{0,16},{1,17},{2,18},{3,19},{4,20},{5,21},{6,22},{7,23},{8,24},{9,... | collective-permute-start | bytes 393224 | tf_op jit(solution)/shard_map/ppermute | solution.py:16
  90.1 0.7 copy-start.3
  93.7 4.4 %collective-permute-start.8 = (f32[8,8,3,1,128]{4,1,3,0,2:T(8,128)S(1)}, f32[8,8,3,1,128]{4,1,3,0,2:T(8,128)S(1)}, u32[]{:S(2)}, u32[]{:S(2)}) collective-permute-start(f32[8,8,3,1,128]{4,1,3,0,2:T(8,128)S(1)} %get-tuple-element.284), channel_id=1, source_target_pairs={{4,0},{8,4},{12,8},{5,1},{9,5},{13,9},{6,2},{10,6},{14,10},{7,3},{... | collective-permute-start | bytes 294920 | tf_op jit(solution)/shard_map/ppermute | solution.py:19
  95.0 4.0 %collective-permute-start.9 = (f32[8,8,3,1,128]{4,1,3,0,2:T(8,128)S(1)}, f32[8,8,3,1,128]{4,1,3,0,2:T(8,128)S(1)}, u32[]{:S(2)}, u32[]{:S(2)}) collective-permute-start(f32[8,8,3,1,128]{4,1,3,0,2:T(8,128)S(1)} %get-tuple-element.283), channel_id=1, source_target_pairs={{0,4},{4,8},{8,12},{1,5},{5,9},{9,13},{2,6},{6,10},{10,14},{3,7},{... | collective-permute-start | bytes 294920 | tf_op jit(solution)/shard_map/ppermute | solution.py:16
  100.1 4.5 %collective-permute-start.11 = (f32[8,8,3,6,1]{1,0,4,3,2:T(8,128)S(1)}, f32[8,8,3,6,1]{1,0,4,3,2:T(8,128)S(1)}, u32[]{:S(2)}, u32[]{:S(2)}) collective-permute-start(f32[8,8,3,6,1]{1,0,4,3,2:T(8,128)S(1)} %copy.218), channel_id=1, source_target_pairs={{0,1},{1,2},{2,3},{4,5},{5,6},{6,7},{8,9},{9,10},{10,11},{12,13},{... | collective-permute-start | bytes 13832 | tf_op jit(solution)/shard_map/ppermute | solution.py:16
  103.2 6.2 %collective-permute-start.10 = (f32[8,8,3,6,1]{1,0,4,3,2:T(8,128)S(1)}, f32[8,8,3,6,1]{1,0,4,3,2:T(8,128)S(1)}, u32[]{:S(2)}, u32[]{:S(2)}) collective-permute-start(f32[8,8,3,6,1]{1,0,4,3,2:T(8,128)S(1)} %copy.216), channel_id=1, source_target_pairs={{1,0},{2,1},{3,2},{5,4},{6,5},{7,6},{9,8},{10,9},{11,10},{13,12},{... | collective-permute-start | bytes 13832 | tf_op jit(solution)/shard_map/ppermute | solution.py:19
  161.4 7.3 %collective-permute-start.12 = (f32[8,8,1,4,128]{4,1,3,0,2:T(8,128)S(1)}, f32[8,8,1,4,128]{4,1,3,0,2:T(8,128)S(1)}, u32[]{:S(2)}, u32[]{:S(2)}) collective-permute-start(f32[8,8,1,4,128]{4,1,3,0,2:T(8,128)S(1)} %bitcast.802), channel_id=1, source_target_pairs={{16,0},{17,1},{18,2},{19,3},{20,4},{21,5},{22,6},{23,7},{24,8},{25... | collective-permute-start | bytes 393224 | tf_op jit(solution)/shard_map/ppermute | solution.py:19
  162.7 7.1 %collective-permute-start.13 = (f32[8,8,1,4,128]{4,1,3,0,2:T(8,128)S(1)}, f32[8,8,1,4,128]{4,1,3,0,2:T(8,128)S(1)}, u32[]{:S(2)}, u32[]{:S(2)}) collective-permute-start(f32[8,8,1,4,128]{4,1,3,0,2:T(8,128)S(1)} %bitcast.803), channel_id=1, source_target_pairs={{0,16},{1,17},{2,18},{3,19},{4,20},{5,21},{6,22},{7,23},{8,24},{9,... | collective-permute-start | bytes 393224 | tf_op jit(solution)/shard_map/ppermute | solution.py:16
  169.8 4.4 %collective-permute-start.14 = (f32[8,8,3,1,128]{4,1,3,0,2:T(8,128)S(1)}, f32[8,8,3,1,128]{4,1,3,0,2:T(8,128)S(1)}, u32[]{:S(2)}, u32[]{:S(2)}) collective-permute-start(f32[8,8,3,1,128]{4,1,3,0,2:T(8,128)S(1)} %get-tuple-element.282), channel_id=1, source_target_pairs={{4,0},{8,4},{12,8},{5,1},{9,5},{13,9},{6,2},{10,6},{14,10},{7,3},{... | collective-permute-start | bytes 294920 | tf_op jit(solution)/shard_map/ppermute | solution.py:19
  171.1 4.0 %collective-permute-start.15 = (f32[8,8,3,1,128]{4,1,3,0,2:T(8,128)S(1)}, f32[8,8,3,1,128]{4,1,3,0,2:T(8,128)S(1)}, u32[]{:S(2)}, u32[]{:S(2)}) collective-permute-start(f32[8,8,3,1,128]{4,1,3,0,2:T(8,128)S(1)} %get-tuple-element.281), channel_id=1, source_target_pairs={{0,4},{4,8},{8,12},{1,5},{5,9},{9,13},{2,6},{6,10},{10,14},{3,7},{... | collective-permute-start | bytes 294920 | tf_op jit(solution)/shard_map/ppermute | solution.py:16
  174.1 0.9 copy-start.2
  176.2 4.5 %collective-permute-start.17 = (f32[8,8,3,6,1]{1,0,4,3,2:T(8,128)S(1)}, f32[8,8,3,6,1]{1,0,4,3,2:T(8,128)S(1)}, u32[]{:S(2)}, u32[]{:S(2)}) collective-permute-start(f32[8,8,3,6,1]{1,0,4,3,2:T(8,128)S(1)} %copy.230), channel_id=1, source_target_pairs={{0,1},{1,2},{2,3},{4,5},{5,6},{6,7},{8,9},{9,10},{10,11},{12,13},{... | collective-permute-start | bytes 13832 | tf_op jit(solution)/shard_map/ppermute | solution.py:16
  179.3 6.2 %collective-permute-start.16 = (f32[8,8,3,6,1]{1,0,4,3,2:T(8,128)S(1)}, f32[8,8,3,6,1]{1,0,4,3,2:T(8,128)S(1)}, u32[]{:S(2)}, u32[]{:S(2)}) collective-permute-start(f32[8,8,3,6,1]{1,0,4,3,2:T(8,128)S(1)} %copy.228), channel_id=1, source_target_pairs={{1,0},{2,1},{3,2},{5,4},{6,5},{7,6},{9,8},{10,9},{11,10},{13,12},{... | collective-permute-start | bytes 13832 | tf_op jit(solution)/shard_map/ppermute | solution.py:19
where the time goes:
time: 247 us; the launch traced here: 246 us
  blocking collectives  129 us (52%)
  starting transfers between devices  42.5 us (17%)
  other arithmetic  23.9 us (10%)
  local copies, waits for them, and re-layouts  18.8 us (8%)
  waiting for transfers between devices  18.3 us (7%)
  matrix products  11.8 us (5%)
    psum x2, blocking collectives, shards(): summed = lax.psum(partial_sums, ('gx', 'gy', 'gz'))  87.7 us
    psum x1, blocking collectives, shards(): lax.psum((pair(rhs, rhs), pair(rhs, raw_image), pair(raw_image, raw_image...  41.6 us
    ppermute x9, starting transfers between devices, with_halo(): lax.ppermute(lax.slice_in_dim(block, block.shape[dim] - width, None, axis...  30.9 us
    ppermute x9, waiting for transfers between devices, with_halo(): lax.ppermute(lax.slice_in_dim(block, 0, width, axis=dim), axis, backward)  14.6 us
    ppermute x9, starting transfers between devices, with_halo(): lax.ppermute(lax.slice_in_dim(block, 0, width, axis=dim), axis, backward)  11.6 us
    another operation x12, other arithmetic, normalizer(): lower = jnp.linalg.cholesky(gram)  5.63 us
    unnamed x14, local copies, waits for them, and re-layouts  5.27 us
    dot_general x11, matrix products, mix(): return jnp.einsum('asxyz,sr->arxyz', field, matrix, precision=HIGH)  4.97 us
  transfers between devices with their start and end apart: 18, of which 8 were waited for; matrix products, arithmetic and copies ran while one was open for 5% of the time, Pallas kernels for 0%

commit v1 on v0

--- a/solution.py
+++ b/solution.py
@@ -80,7 +80,8 @@
         else:
             stacked = jnp.stack(basis + [image])
             partial_sums = jnp.einsum("karxyz,asxyz->krs", stacked, image, precision=HIGH)
-            summed = lax.psum(partial_sums, ("gx", "gy", "gz"))
+            half = lax.psum(partial_sums, ("gy", "gz"))
+            summed = lax.psum(half, "gx")
             coeffs = [summed[index] for index in range(len(basis))]
             gram = summed[len(basis)]
         rest = image

time: 247 us -> 296 us (1.20)
  blocking collectives: 129 us -> 177 us
    psum x2 -> x4, blocking collectives: 87.7 us -> 136 us  [the longest x2 120 us: shards(): half = lax.psum(partial_sums, ('gy', 'gz'))]
  transfers between devices with their start and end apart: 18 -> 18, of which waited for: 8 -> 8; matrix products, arithmetic and copies ran while one was open for 5% -> 4% of each run, Pallas kernels for 0% -> 0%
where the time goes in v1:
time: 296 us; the launch traced here: 293 us
  blocking collectives  177 us (60%)
  starting transfers between devices  41.7 us (14%)
  other arithmetic  23.7 us (8%)
  local copies, waits for them, and re-layouts  18.7 us (6%)
  waiting for transfers between devices  18.3 us (6%)
  matrix products  11.8 us (4%)
    psum x2, blocking collectives, shards(): half = lax.psum(partial_sums, ('gy', 'gz'))  120 us
    psum x1, blocking collectives, shards(): lax.psum((pair(rhs, rhs), pair(rhs, raw_image), pair(raw_image, raw_image...  41.6 us
    ppermute x9, starting transfers between devices, with_halo(): lax.ppermute(lax.slice_in_dim(block, block.shape[dim] - width, None, axis...  30 us
    psum x2, blocking collectives, shards(): summed = lax.psum(half, 'gx')  16 us
    ppermute x9, waiting for transfers between devices, with_halo(): lax.ppermute(lax.slice_in_dim(block, 0, width, axis=dim), axis, backward)  14.6 us
    ppermute x9, starting transfers between devices, with_halo(): lax.ppermute(lax.slice_in_dim(block, 0, width, axis=dim), axis, backward)  11.6 us
  transfers between devices with their start and end apart: 18, of which 8 were waited for; matrix products, arithmetic and copies ran while one was open for 4% of the time, Pallas kernels for 0%

profile of v1, /device:TPU:0, one launch (start us, length us, event | category | flops | bytes accessed | tf_op | source)
XLA Modules:
  0.0 293.0 jit_solution(1551030800274486974)
XLA Ops:
  0.6 1.0 copy.203
  1.6 4.9 %collective-permute-start.1 = (f32[8,8,1,4,128]{4,1,3,2,0:T(8,128)S(1)}, f32[8,8,1,4,128]{4,1,3,2,0:T(8,128)S(1)}, u32[]{:S(2)}, u32[]{:S(2)}) collective-permute-start(f32[8,8,1,4,128]{4,1,3,2,0:T(8,128)S(1)} %copy.203), channel_id=1, source_target_pairs={{0,16},{1,17},{2,18},{3,19},{4,20},{5,21},{6,22},{7,23},{8,24},{9,... | collective-permute-start | bytes 393224 | tf_op jit(solution)/shard_map/ppermute | solution.py:16
  6.5 1.3 collective-permute-start
  10.2 3.1 %collective-permute-done = f32[8,8,1,4,128]{4,1,3,2,0:T(8,128)S(1)} collective-permute-done((f32[8,8,1,4,128]{4,1,3,2,0:T(8,128)S(1)}, f32[8,8,1,4,128]{4,1,3,2,0:T(8,128)S(1)}, u32[]{:S(2)}, u32[]{:S(2)}) %collective-permute-start) | collective-permute-done | bytes 131104 | tf_op jit(solution)/shard_map/ppermute | solution.py:19
  13.4 1.3 collective-permute-start.2
  14.7 3.0 %collective-permute-start.3 = (f32[8,8,3,1,128]{4,1,3,2,0:T(8,128)S(1)}, f32[8,8,3,1,128]{4,1,3,2,0:T(8,128)S(1)}, u32[]{:S(2)}, u32[]{:S(2)}) collective-permute-start(f32[8,8,3,1,128]{4,1,3,2,0:T(8,128)S(1)} %get-tuple-element.285), channel_id=1, source_target_pairs={{0,4},{4,8},{8,12},{1,5},{5,9},{9,13},{2,6},{6,10},{10,14},{3,7},{... | collective-permute-start | bytes 294920 | tf_op jit(solution)/shard_map/ppermute | solution.py:16
  19.8 3.5 %collective-permute-start.5 = (f32[8,8,3,6,1]{1,0,4,3,2:T(8,128)S(1)}, f32[8,8,3,6,1]{1,0,4,3,2:T(8,128)S(1)}, u32[]{:S(2)}, u32[]{:S(2)}) collective-permute-start(f32[8,8,3,6,1]{1,0,4,3,2:T(8,128)S(1)} %copy.278), channel_id=1, source_target_pairs={{0,1},{1,2},{2,3},{4,5},{5,6},{6,7},{8,9},{9,10},{10,11},{12,13},{... | collective-permute-start | bytes 13832 | tf_op jit(solution)/shard_map/ppermute | solution.py:16
  24.2 1.3 collective-permute-start.4
  25.6 0.9 copy.209
  26.7 4.0 %collective-permute-done.4 = f32[8,8,3,6,1]{1,0,4,3,2:T(8,128)S(1)} collective-permute-done((f32[8,8,3,6,1]{1,0,4,3,2:T(8,128)S(1)}, f32[8,8,3,6,1]{1,0,4,3,2:T(8,128)S(1)}, u32[]{:S(2)}, u32[]{:S(2)}) %collective-permute-start.4) | collective-permute-done | bytes 4640 | tf_op jit(solution)/shard_map/ppermute | solution.py:19
  30.7 0.9 copy.207
  31.8 1.0 multiply_add_fusion.2
  33.6 41.6 %all-reduce.1 = (f32[8,8]{0,1:T(8,128)S(1)}, f32[8,8]{1,0:T(8,128)S(1)}, f32[8,8]{0,1:T(8,128)S(1)}) all-reduce(f32[8,8]{0,1:T(8,128)S(1)} %convolution_bitcast_fusion.13, f32[8,8]{1,0:T(8,128)S(1)} %convolution_bitcast_fusion.12, f32[8,8]{0,1:T(8,128)S(1)} %convolution_bitcast_fusion.11), channel_id=1, replica_groups=mesh['gx'=2,'gy'=4,'gz'=4] {'gx','gy','gz'}, use_global_device_ids=true, to_apply=%region_0.0 | all-reduce | flops 192 | bytes 1536 | tf_op jit(solution)/shard_map/psum | solution.py:66
  83.0 1.3 collective-permute-start.6
  84.3 4.6 %collective-permute-start.7 = (f32[8,8,1,4,128]{4,1,3,0,2:T(8,128)S(1)}, f32[8,8,1,4,128]{4,1,3,0,2:T(8,128)S(1)}, u32[]{:S(2)}, u32[]{:S(2)}) collective-permute-start(f32[8,8,1,4,128]{4,1,3,0,2:T(8,128)S(1)} %bitcast.786), channel_id=1, source_target_pairs={{0,16},{1,17},{2,18},{3,19},{4,20},{5,21},{6,22},{7,23},{8,24},{9,... | collective-permute-start | bytes 393224 | tf_op jit(solution)/shard_map/ppermute | solution.py:16
  90.8 2.7 and_reduce_fusion
  93.5 1.3 collective-permute-start.8
  94.8 3.0 %collective-permute-start.9 = (f32[8,8,3,1,128]{4,1,3,0,2:T(8,128)S(1)}, f32[8,8,3,1,128]{4,1,3,0,2:T(8,128)S(1)}, u32[]{:S(2)}, u32[]{:S(2)}) collective-permute-start(f32[8,8,3,1,128]{4,1,3,0,2:T(8,128)S(1)} %get-tuple-element.283), channel_id=1, source_target_pairs={{0,4},{4,8},{8,12},{1,5},{5,9},{9,13},{2,6},{6,10},{10,14},{3,7},{... | collective-permute-start | bytes 294920 | tf_op jit(solution)/shard_map/ppermute | solution.py:16
  99.1 0.9 copy.218
  100.0 2.2 collective-permute-start.11
  103.0 1.3 collective-permute-start.10
  104.4 0.9 copy.219
  105.6 3.7 %collective-permute-done.10 = f32[8,8,3,6,1]{1,0,4,3,2:T(8,128)S(1)} collective-permute-done((f32[8,8,3,6,1]{1,0,4,3,2:T(8,128)S(1)}, f32[8,8,3,6,1]{1,0,4,3,2:T(8,128)S(1)}, u32[]{:S(2)}, u32[]{:S(2)}) %collective-permute-start.10) | collective-permute-done | bytes 4640 | tf_op jit(solution)/shard_map/ppermute | solution.py:19
  109.3 0.9 copy.217
  110.5 1.1 multiply_add_fusion.1
  111.5 1.6 convolution_bitcast_fusion.7
  113.2 60.0 %psum.52 = f32[3,8,8]{2,1,0:T(8,128)S(1)} all-reduce(f32[3,8,8]{2,1,0:T(8,128)S(1)} %convolution_bitcast_fusion.7), channel_id=1, replica_groups=mesh['gx'=2,'gy'=4,'gz'=4] {'gy','gz'}, use_global_device_ids=true, to_apply=%region_5.8 | all-reduce | flops 192 | bytes 1536 | tf_op jit(solution)/shard_map/psum | solution.py:83
  173.2 6.9 %psum.53 = f32[3,8,8]{2,1,0:T(8,128)S(1)} all-reduce(f32[3,8,8]{2,1,0:T(8,128)S(1)} %psum.52), channel_id=1, replica_groups=mesh['gx'=2,'gy'=4,'gz'=4] {'gx'}, use_global_device_ids=true, to_apply=%region_6.9 | all-reduce | flops 192 | bytes 1536 | tf_op jit(solution)/shard_map/psum | solution.py:84
  183.8 1.3 fusion.3
  185.4 1.3 collective-permute-start.12
  186.7 4.6 %collective-permute-start.13 = (f32[8,8,1,4,128]{4,1,3,0,2:T(8,128)S(1)}, f32[8,8,1,4,128]{4,1,3,0,2:T(8,128)S(1)}, u32[]{:S(2)}, u32[]{:S(2)}) collective-permute-start(f32[8,8,1,4,128]{4,1,3,0,2:T(8,128)S(1)} %bitcast.803), channel_id=1, source_target_pairs={{0,16},{1,17},{2,18},{3,19},{4,20},{5,21},{6,22},{7,23},{8,24},{9,... | collective-permute-start | bytes 393224 | tf_op jit(solution)/shard_map/ppermute | solution.py:16
  191.3 1.3 fusion.499
  192.7 1.1 collective-permute-done.13
  193.8 1.3 collective-permute-start.14
  195.1 3.0 %collective-permute-start.15 = (f32[8,8,3,1,128]{4,1,3,0,2:T(8,128)S(1)}, f32[8,8,3,1,128]{4,1,3,0,2:T(8,128)S(1)}, u32[]{:S(2)}, u32[]{:S(2)}) collective-permute-start(f32[8,8,3,1,128]{4,1,3,0,2:T(8,128)S(1)} %get-tuple-element.281), channel_id=1, source_target_pairs={{0,4},{4,8},{8,12},{1,5},{5,9},{9,13},{2,6},{6,10},{10,14},{3,7},{... | collective-permute-start | bytes 294920 | tf_op jit(solution)/shard_map/ppermute | solution.py:16
  199.3 0.9 copy.230
  200.2 1.3 collective-permute-start.17
  202.4 1.3 collective-permute-start.16
  203.8 0.9 copy.231
  205.0 3.7 %collective-permute-done.16 = f32[8,8,3,6,1]{1,0,4,3,2:T(8,128)S(1)} collective-permute-done((f32[8,8,3,6,1]{1,0,4,3,2:T(8,128)S(1)}, f32[8,8,3,6,1]{1,0,4,3,2:T(8,128)S(1)}, u32[]{:S(2)}, u32[]{:S(2)}) %collective-permute-start.16) | collective-permute-done | bytes 4640 | tf_op jit(solution)/shard_map/ppermute | solution.py:19
  208.7 0.9 copy.229
  209.9 1.0 multiply_add_fusion
  210.9 1.6 convolution_bitcast_fusion.6
  212.5 59.7 %psum.54 = f32[4,8,8]{2,1,0:T(8,128)S(1)} all-reduce(f32[4,8,8]{2,1,0:T(8,128)S(1)} %convolution_bitcast_fusion.6), channel_id=1, replica_groups=mesh['gx'=2,'gy'=4,'gz'=4] {'gy','gz'}, use_global_device_ids=true, to_apply=%region_7.10 | all-reduce | flops 256 | bytes 2048 | tf_op jit(solution)/shard_map/psum | solution.py:83
  272.2 9.1 %psum.55 = f32[4,8,8]{2,1,0:T(8,128)S(1)} all-reduce(f32[4,8,8]{2,1,0:T(8,128)S(1)} %psum.54), channel_id=1, replica_groups=mesh['gx'=2,'gy'=4,'gz'=4] {'gx'}, use_global_device_ids=true, to_apply=%region_8.11 | all-reduce | flops 256 | bytes 2048 | tf_op jit(solution)/shard_map/psum | solution.py:84
  285.6 1.1 fusion.7
  287.0 0.9 copy.245
  287.9 3.2 %fusion.498 = f32[4,8,3,8]{3,1,2,0:T(8,128)} fusion(f32[4,8,3,8]{3,1,2,0:T(8,128)} %copy-done.2, s32[]{:T(128)} %bitcast.379, s32[]{:T(128)} %bitcast.380, f32[4,8,8]{2,1,0:T(8,128)S(1)} %psum.55, pred[]{:T(512)} %get-tuple-element.118), kind=kLoop, calls=%fused_computation.797 | loop fusion | flops 64 | bytes 9984 | tf_op jit(solution)/shard_map/scatter | solution.py:95
  (151 shorter events, 31.8 us)
Async XLA Ops:
  0.6 8.1 %copy-start.1 = (bf16[7,8,8,1,4,128]{5,4,3,2,1,0:T(4,128)(2,1)S(1)}, bf16[7,8,8,1,4,128]{5,4,3,2,1,0:T(4,128)(2,1)}, u32[]{:S(2)}) copy-start(bf16[7,8,8,1,4,128]{5,4,3,2,1,0:T(4,128)(2,1)} %param.24) | copy-start | bytes 1376260
  1.6 8.5 %collective-permute-start.1 = (f32[8,8,1,4,128]{4,1,3,2,0:T(8,128)S(1)}, f32[8,8,1,4,128]{4,1,3,2,0:T(8,128)S(1)}, u32[]{:S(2)}, u32[]{:S(2)}) collective-permute-start(f32[8,8,1,4,128]{4,1,3,2,0:T(8,128)S(1)} %copy.203), channel_id=1, source_target_pairs={{0,16},{1,17},{2,18},{3,19},{4,20},{5,21},{6,22},{7,23},{8,24},{9,... | collective-permute-start | bytes 393224 | tf_op jit(solution)/shard_map/ppermute | solution.py:16
  6.5 6.9 %collective-permute-start = (f32[8,8,1,4,128]{4,1,3,2,0:T(8,128)S(1)}, f32[8,8,1,4,128]{4,1,3,2,0:T(8,128)S(1)}, u32[]{:S(2)}, u32[]{:S(2)}) collective-permute-start(f32[8,8,1,4,128]{4,1,3,2,0:T(8,128)S(1)} %copy.203), channel_id=1, source_target_pairs={{16,0},{17,1},{18,2},{19,3},{20,4},{21,5},{22,6},{23,7},{24,8},{25... | collective-permute-start | bytes 393224 | tf_op jit(solution)/shard_map/ppermute | solution.py:19
  8.8 0.9 copy-start
  13.4 4.4 %collective-permute-start.2 = (f32[8,8,3,1,128]{4,1,3,2,0:T(8,128)S(1)}, f32[8,8,3,1,128]{4,1,3,2,0:T(8,128)S(1)}, u32[]{:S(2)}, u32[]{:S(2)}) collective-permute-start(f32[8,8,3,1,128]{4,1,3,2,0:T(8,128)S(1)} %get-tuple-element.286), channel_id=1, source_target_pairs={{4,0},{8,4},{12,8},{5,1},{9,5},{13,9},{6,2},{10,6},{14,10},{7,3},{... | collective-permute-start | bytes 294920 | tf_op jit(solution)/shard_map/ppermute | solution.py:19
  14.7 4.0 %collective-permute-start.3 = (f32[8,8,3,1,128]{4,1,3,2,0:T(8,128)S(1)}, f32[8,8,3,1,128]{4,1,3,2,0:T(8,128)S(1)}, u32[]{:S(2)}, u32[]{:S(2)}) collective-permute-start(f32[8,8,3,1,128]{4,1,3,2,0:T(8,128)S(1)} %get-tuple-element.285), channel_id=1, source_target_pairs={{0,4},{4,8},{8,12},{1,5},{5,9},{9,13},{2,6},{6,10},{10,14},{3,7},{... | collective-permute-start | bytes 294920 | tf_op jit(solution)/shard_map/ppermute | solution.py:16
  19.8 5.7 %collective-permute-start.5 = (f32[8,8,3,6,1]{1,0,4,3,2:T(8,128)S(1)}, f32[8,8,3,6,1]{1,0,4,3,2:T(8,128)S(1)}, u32[]{:S(2)}, u32[]{:S(2)}) collective-permute-start(f32[8,8,3,6,1]{1,0,4,3,2:T(8,128)S(1)} %copy.278), channel_id=1, source_target_pairs={{0,1},{1,2},{2,3},{4,5},{5,6},{6,7},{8,9},{9,10},{10,11},{12,13},{... | collective-permute-start | bytes 13832 | tf_op jit(solution)/shard_map/ppermute | solution.py:16
  24.2 6.5 %collective-permute-start.4 = (f32[8,8,3,6,1]{1,0,4,3,2:T(8,128)S(1)}, f32[8,8,3,6,1]{1,0,4,3,2:T(8,128)S(1)}, u32[]{:S(2)}, u32[]{:S(2)}) collective-permute-start(f32[8,8,3,6,1]{1,0,4,3,2:T(8,128)S(1)} %copy.277), channel_id=1, source_target_pairs={{1,0},{2,1},{3,2},{5,4},{6,5},{7,6},{9,8},{10,9},{11,10},{13,12},{... | collective-permute-start | bytes 13832 | tf_op jit(solution)/shard_map/ppermute | solution.py:19
  83.0 10.5 %collective-permute-start.6 = (f32[8,8,1,4,128]{4,1,3,0,2:T(8,128)S(1)}, f32[8,8,1,4,128]{4,1,3,0,2:T(8,128)S(1)}, u32[]{:S(2)}, u32[]{:S(2)}) collective-permute-start(f32[8,8,1,4,128]{4,1,3,0,2:T(8,128)S(1)} %bitcast.785), channel_id=1, source_target_pairs={{16,0},{17,1},{18,2},{19,3},{20,4},{21,5},{22,6},{23,7},{24,8},{25... | collective-permute-start | bytes 393224 | tf_op jit(solution)/shard_map/ppermute | solution.py:19
  84.3 9.2 %collective-permute-start.7 = (f32[8,8,1,4,128]{4,1,3,0,2:T(8,128)S(1)}, f32[8,8,1,4,128]{4,1,3,0,2:T(8,128)S(1)}, u32[]{:S(2)}, u32[]{:S(2)}) collective-permute-start(f32[8,8,1,4,128]{4,1,3,0,2:T(8,128)S(1)} %bitcast.786), channel_id=1, source_target_pairs={{0,16},{1,17},{2,18},{3,19},{4,20},{5,21},{6,22},{7,23},{8,24},{9,... | collective-permute-start | bytes 393224 | tf_op jit(solution)/shard_map/ppermute | solution.py:16
  90.1 0.7 copy-start.3
  93.5 4.4 %collective-permute-start.8 = (f32[8,8,3,1,128]{4,1,3,0,2:T(8,128)S(1)}, f32[8,8,3,1,128]{4,1,3,0,2:T(8,128)S(1)}, u32[]{:S(2)}, u32[]{:S(2)}) collective-permute-start(f32[8,8,3,1,128]{4,1,3,0,2:T(8,128)S(1)} %get-tuple-element.284), channel_id=1, source_target_pairs={{4,0},{8,4},{12,8},{5,1},{9,5},{13,9},{6,2},{10,6},{14,10},{7,3},{... | collective-permute-start | bytes 294920 | tf_op jit(solution)/shard_map/ppermute | solution.py:19
  94.8 4.0 %collective-permute-start.9 = (f32[8,8,3,1,128]{4,1,3,0,2:T(8,128)S(1)}, f32[8,8,3,1,128]{4,1,3,0,2:T(8,128)S(1)}, u32[]{:S(2)}, u32[]{:S(2)}) collective-permute-start(f32[8,8,3,1,128]{4,1,3,0,2:T(8,128)S(1)} %get-tuple-element.283), channel_id=1, source_target_pairs={{0,4},{4,8},{8,12},{1,5},{5,9},{9,13},{2,6},{6,10},{10,14},{3,7},{... | collective-permute-start | bytes 294920 | tf_op jit(solution)/shard_map/ppermute | solution.py:16
  100.0 4.5 %collective-permute-start.11 = (f32[8,8,3,6,1]{1,0,4,3,2:T(8,128)S(1)}, f32[8,8,3,6,1]{1,0,4,3,2:T(8,128)S(1)}, u32[]{:S(2)}, u32[]{:S(2)}) collective-permute-start(f32[8,8,3,6,1]{1,0,4,3,2:T(8,128)S(1)} %copy.218), channel_id=1, source_target_pairs={{0,1},{1,2},{2,3},{4,5},{5,6},{6,7},{8,9},{9,10},{10,11},{12,13},{... | collective-permute-start | bytes 13832 | tf_op jit(solution)/shard_map/ppermute | solution.py:16
  103.0 6.2 %collective-permute-start.10 = (f32[8,8,3,6,1]{1,0,4,3,2:T(8,128)S(1)}, f32[8,8,3,6,1]{1,0,4,3,2:T(8,128)S(1)}, u32[]{:S(2)}, u32[]{:S(2)}) collective-permute-start(f32[8,8,3,6,1]{1,0,4,3,2:T(8,128)S(1)} %copy.216), channel_id=1, source_target_pairs={{1,0},{2,1},{3,2},{5,4},{6,5},{7,6},{9,8},{10,9},{11,10},{13,12},{... | collective-permute-start | bytes 13832 | tf_op jit(solution)/shard_map/ppermute | solution.py:19
  185.4 7.3 %collective-permute-start.12 = (f32[8,8,1,4,128]{4,1,3,0,2:T(8,128)S(1)}, f32[8,8,1,4,128]{4,1,3,0,2:T(8,128)S(1)}, u32[]{:S(2)}, u32[]{:S(2)}) collective-permute-start(f32[8,8,1,4,128]{4,1,3,0,2:T(8,128)S(1)} %bitcast.802), channel_id=1, source_target_pairs={{16,0},{17,1},{18,2},{19,3},{20,4},{21,5},{22,6},{23,7},{24,8},{25... | collective-permute-start | bytes 393224 | tf_op jit(solution)/shard_map/ppermute | solution.py:19
  186.7 7.1 %collective-permute-start.13 = (f32[8,8,1,4,128]{4,1,3,0,2:T(8,128)S(1)}, f32[8,8,1,4,128]{4,1,3,0,2:T(8,128)S(1)}, u32[]{:S(2)}, u32[]{:S(2)}) collective-permute-start(f32[8,8,1,4,128]{4,1,3,0,2:T(8,128)S(1)} %bitcast.803), channel_id=1, source_target_pairs={{0,16},{1,17},{2,18},{3,19},{4,20},{5,21},{6,22},{7,23},{8,24},{9,... | collective-permute-start | bytes 393224 | tf_op jit(solution)/shard_map/ppermute | solution.py:16
  193.8 4.4 %collective-permute-start.14 = (f32[8,8,3,1,128]{4,1,3,0,2:T(8,128)S(1)}, f32[8,8,3,1,128]{4,1,3,0,2:T(8,128)S(1)}, u32[]{:S(2)}, u32[]{:S(2)}) collective-permute-start(f32[8,8,3,1,128]{4,1,3,0,2:T(8,128)S(1)} %get-tuple-element.282), channel_id=1, source_target_pairs={{4,0},{8,4},{12,8},{5,1},{9,5},{13,9},{6,2},{10,6},{14,10},{7,3},{... | collective-permute-start | bytes 294920 | tf_op jit(solution)/shard_map/ppermute | solution.py:19
  195.1 4.0 %collective-permute-start.15 = (f32[8,8,3,1,128]{4,1,3,0,2:T(8,128)S(1)}, f32[8,8,3,1,128]{4,1,3,0,2:T(8,128)S(1)}, u32[]{:S(2)}, u32[]{:S(2)}) collective-permute-start(f32[8,8,3,1,128]{4,1,3,0,2:T(8,128)S(1)} %get-tuple-element.281), channel_id=1, source_target_pairs={{0,4},{4,8},{8,12},{1,5},{5,9},{9,13},{2,6},{6,10},{10,14},{3,7},{... | collective-permute-start | bytes 294920 | tf_op jit(solution)/shard_map/ppermute | solution.py:16
  198.1 0.9 copy-start.2
  200.2 3.6 %collective-permute-start.17 = (f32[8,8,3,6,1]{1,0,4,3,2:T(8,128)S(1)}, f32[8,8,3,6,1]{1,0,4,3,2:T(8,128)S(1)}, u32[]{:S(2)}, u32[]{:S(2)}) collective-permute-start(f32[8,8,3,6,1]{1,0,4,3,2:T(8,128)S(1)} %copy.230), channel_id=1, source_target_pairs={{0,1},{1,2},{2,3},{4,5},{5,6},{6,7},{8,9},{9,10},{10,11},{12,13},{... | collective-permute-start | bytes 13832 | tf_op jit(solution)/shard_map/ppermute | solution.py:16
  202.4 6.2 %collective-permute-start.16 = (f32[8,8,3,6,1]{1,0,4,3,2:T(8,128)S(1)}, f32[8,8,3,6,1]{1,0,4,3,2:T(8,128)S(1)}, u32[]{:S(2)}, u32[]{:S(2)}) collective-permute-start(f32[8,8,3,6,1]{1,0,4,3,2:T(8,128)S(1)} %copy.228), channel_id=1, source_target_pairs={{1,0},{2,1},{3,2},{5,4},{6,5},{7,6},{9,8},{10,9},{11,10},{13,12},{... | collective-permute-start | bytes 13832 | tf_op jit(solution)/shard_map/ppermute | solution.py:19
